TPU v7x, 32 devices: a whole 2x2x4 slice. The times are simulated.
32 devices in a mesh: seq: 8 (over z, x), head: 4 (over y, core).
Axes of the slice: x: 2, y: 2, z: 4, core: 2. Of those that a mesh axis runs over, the one named last changes fastest.
Arguments:
- queries: bfloat16 [8192, 4096], P('seq', 'head'), may hold values from -150 to 150
- keys: bfloat16 [8192, 4096], P('seq', 'head'), may hold values from -7 to 7
- values: bfloat16 [8192, 4096], P('seq', 'head'), may hold values from -6 to 6
- random_holder: int32 [32, 64, 3], P('head', 'seq'), may hold values from 0 to 7, all different within a row; in each aligned block of 8 rows (0 to 7, 8 to 15, ..., all dimensions but the last counted through in order) at most 3 rows name the same one
- random_offset: int32 [32, 64, 3], P('head', 'seq'), may hold values from 0 to 7
- keep: int32 [64], P('seq'), may hold values from 0 to 1, as said below
Outputs:
- packed: bfloat16 [8192, 4096], P('seq', 'head')
Inputs may be any that keep to these rules, and one draw needn't show every extreme that they name: `random_holder`: for each head, the 8 query blocks of one index of seq name no index of seq more than 3 times over all their random entries; the 3 entries of one query block and head differ. `keep`: block j is kept where j % 8 == 0 or j % 8 == 7, and not kept where j % 8 == 1.
All inputs are finite; a program needn't handle non-finite values.
Results may differ from a plain program's by a relative error of at most 0.007.
Values may be sent and summed in bfloat16 or wider, within the bound.
A program may use at most 128 MiB of HBM per device.

v0:
```python
import functools
import math

import jax
import jax.numpy as jnp
from jax import lax
from jax.experimental import pallas as pl
from jax.experimental.pallas import tpu as pltpu
from jax.sharding import PartitionSpec as P

DH = 128
B = 128
G = 2
R = 3

neg_big = -1e30
ANYWHERE = pltpu.CompilerParams(
    dimension_semantics=("arbitrary",), vmem_limit_bytes=60 * 1024 * 1024
)


def halo(block, axis, width):
    count = lax.axis_size(axis)
    forward = [(i, i + 1) for i in range(count - 1)]
    backward = [(target, source) for source, target in forward]
    low = lax.ppermute(block[-width:], axis, forward)
    high = lax.ppermute(block[:width], axis, backward)
    return jnp.concatenate([low, high], axis=0)


def broadcast(block, axis, source):
    block = jnp.where(lax.axis_index(axis) == source, block, jnp.zeros_like(block))
    return lax.psum(block, axis)


def pick_kernel(cap, head_ref, block_ref, k_ref, v_ref, out_ref):
    dest = pl.program_id(0)

    @pl.loop(0, cap)
    def _(j):
        rows = pl.ds(pl.multiple_of(block_ref[dest, j] * B, B), B)
        cols = pl.ds(pl.multiple_of(head_ref[dest, j] * DH, DH), DH)
        out_ref[j, 0] = k_ref[rows, cols]
        out_ref[j, 1] = v_ref[rows, cols]


def pick(keys, values, heads, blocks, seq_count, cap):
    whole = pl.BlockSpec(keys.shape, lambda d, *_: (0, 0))
    return pl.pallas_call(
        functools.partial(pick_kernel, cap),
        out_shape=jax.ShapeDtypeStruct((seq_count * cap, 2, B, DH), keys.dtype),
        grid_spec=pltpu.PrefetchScalarGridSpec(
            num_scalar_prefetch=2,
            grid=(seq_count,),
            in_specs=[whole, whole],
            out_specs=pl.BlockSpec((cap, 2, B, DH), lambda d, *_: (d, 0, 0, 0)),
        ),
        compiler_params=ANYWHERE,
    )(heads, blocks, keys, values)


def attend_kernel(
    blk_dev,
    keep_ref,
    slot_ref,
    live_ref,
    where_ref,
    q_ref,
    k_ref,
    v_ref,
    hk_ref,
    hv_ref,
    gk_ref,
    gv_ref,
    rand_ref,
    out_ref,
):
    scale = 1.0 / math.sqrt(DH)
    head = pl.program_id(0)
    out_ref[...] = jnp.zeros_like(out_ref)

    def tile(ref, halo_ref, i):
        if i < 0:
            return halo_ref[:B]
        if i >= blk_dev:
            return halo_ref[B:]
        return ref[i * B : (i + 1) * B]

    def one(i):
        q = q_ref[i * B : (i + 1) * B]
        near = range(i - 1, i + 2)
        picks = [where_ref[(head * blk_dev + i) * R + r] for r in range(R)]
        k_parts = [
            jnp.concatenate([tile(k_ref, hk_ref, n) for n in near], axis=0),
            gk_ref[...],
            jnp.concatenate([rand_ref[p, 0] for p in picks], axis=0),
        ]
        v_parts = [
            jnp.concatenate([tile(v_ref, hv_ref, n) for n in near], axis=0),
            gv_ref[...],
            jnp.concatenate([rand_ref[p, 1] for p in picks], axis=0),
        ]
        scores = [
            lax.dot_general(
                q, k, (((1,), (1,)), ((), ())), preferred_element_type=jnp.float32
            )
            * scale
            for k in k_parts
        ]
        lanes = lax.broadcasted_iota(jnp.int32, scores[0].shape, 1)
        if i == 0:
            dead = jnp.logical_and(lanes < B, live_ref[0] == 0)
            scores[0] = jnp.where(dead, neg_big, scores[0])
        if i == blk_dev - 1:
            dead = jnp.logical_and(lanes >= 2 * B, live_ref[1] == 0)
            scores[0] = jnp.where(dead, neg_big, scores[0])
        peak = functools.reduce(
            jnp.maximum, [jnp.max(s, axis=-1, keepdims=True) for s in scores]
        )
        numer = jnp.zeros((B, DH), jnp.float32)
        denom = jnp.zeros((B, 1), jnp.float32)
        for s, v in zip(scores, v_parts):
            w = jnp.exp(s - peak).astype(jnp.bfloat16)
            denom = denom + jnp.sum(w.astype(jnp.float32), axis=-1, keepdims=True)
            numer = numer + jnp.dot(w, v, preferred_element_type=jnp.float32)
        rows = pl.ds(pl.multiple_of(slot_ref[i] * B, B), B)
        out_ref[rows, :] = (numer / denom).astype(out_ref.dtype)

    for i in range(blk_dev):
        pl.when(keep_ref[i] > 0)(functools.partial(one, i))


def attend(keep, slot, live, where, q, k, v, hk, hv, gk, gv, rand):
    tok_dev, width_dev = q.shape
    blk_dev, head_dev = tok_dev // B, width_dev // DH

    def column(rows):
        return pl.BlockSpec((rows, DH), lambda h, *_: (0, h))

    return pl.pallas_call(
        functools.partial(attend_kernel, blk_dev),
        out_shape=jax.ShapeDtypeStruct(q.shape, q.dtype),
        grid_spec=pltpu.PrefetchScalarGridSpec(
            num_scalar_prefetch=4,
            grid=(head_dev,),
            in_specs=[column(tok_dev)] * 3
            + [column(2 * B)] * 2
            + [column(G * B)] * 2
            + [pl.BlockSpec(rand.shape, lambda h, *_: (0, 0, 0, 0))],
            out_specs=column(tok_dev),
        ),
        compiler_params=ANYWHERE,
    )(keep, slot, live, where, q, k, v, hk, hv, gk, gv, rand)


def copy_kernel(order_ref, in_ref, out_ref):
    out_ref[...] = in_ref[...]


def take_blocks(blocks, order, cap):
    width = blocks.shape[1]
    return pl.pallas_call(
        copy_kernel,
        out_shape=jax.ShapeDtypeStruct((cap * B, width), blocks.dtype),
        grid_spec=pltpu.PrefetchScalarGridSpec(
            num_scalar_prefetch=1,
            grid=(cap,),
            in_specs=[pl.BlockSpec((B, width), lambda j, order: (order[j], 0))],
            out_specs=pl.BlockSpec((B, width), lambda j, order: (j, 0)),
        ),
        compiler_params=ANYWHERE,
    )(order, blocks)


def merge_kernel(kind_ref, from_ref, old_ref, new_ref, out_ref):
    kind = kind_ref[pl.program_id(0)]

    @pl.when(kind == 0)
    def _():
        out_ref[...] = old_ref[...]

    @pl.when(kind == 1)
    def _():
        out_ref[...] = jnp.zeros_like(out_ref)

    @pl.when(kind == 2)
    def _():
        out_ref[...] = new_ref[...]


def merge_blocks(old, new, kind, place):
    tok_dev, width = old.shape
    return pl.pallas_call(
        merge_kernel,
        out_shape=jax.ShapeDtypeStruct(old.shape, old.dtype),
        grid_spec=pltpu.PrefetchScalarGridSpec(
            num_scalar_prefetch=2,
            grid=(tok_dev // B,),
            in_specs=[
                pl.BlockSpec((B, width), lambda j, kind, place: (j, 0)),
                pl.BlockSpec((B, width), lambda j, kind, place: (place[j], 0)),
            ],
            out_specs=pl.BlockSpec((B, width), lambda j, kind, place: (j, 0)),
        ),
        compiler_params=ANYWHERE,
    )(kind, place, old, new)


def exclusive(flags, axis):
    return jnp.cumsum(flags, axis=axis) - flags


def first_at_least(caps, amount):
    return jnp.sum((amount > jnp.asarray(caps, jnp.int32)).astype(jnp.int32))


def settle(blocks, keep_all, slot, source, distance, me, count, blk_dev):
    i32 = jnp.int32
    devices = jnp.arange(count, dtype=i32)
    slots = jnp.arange(blk_dev, dtype=i32)
    sizes = sorted({0, *range(blk_dev // 2, blk_dev - 1), blk_dev})
    for bit_pos in range((count - 1).bit_length()):
        stride = 2**bit_pos
        at = source - distance % stride
        moving = (keep_all > 0) & (distance // stride % 2 > 0)
        on_slot = ((slot[:, None] == slots) & moving[:, None]).astype(i32)
        on_device = (at[:, None] == devices).astype(i32)
        leaving = jnp.sum(on_device[:, :, None] * on_slot[:, None, :], axis=0)
        needed = jnp.max(jnp.sum(leaving, axis=1))
        nth = exclusive(leaving, 1)
        mine_out, mine_nth = leaving[me], nth[me]
        send = jnp.sum(
            mine_out[:, None] * (mine_nth[:, None] == slots).astype(i32) * slots[:, None], axis=0
        )
        far = jnp.minimum(me + stride, count - 1)
        comes = jnp.where(me + stride < count, leaving[far], 0)
        kind = jnp.where(comes > 0, 2, jnp.where(mine_out > 0, 1, 0)).astype(i32)
        place = jnp.where(comes > 0, nth[far], 0)
        all_pairs = [(i, i - stride) for i in range(stride, count)]
        split = count - stride // 2
        upper = [pair for pair in all_pairs if pair[0] >= split]
        halves = 2 * stride >= count and 0 < len(upper) < len(all_pairs)

        def shifting(cap, pairs, send=send, kind=kind, place=place):
            def run(blocks):
                if cap == 0:
                    return blocks
                moved = lax.ppermute(take_blocks(blocks, send, cap), "seq", pairs)
                return merge_blocks(blocks, moved, kind, jnp.minimum(place, cap - 1))

            return run

        which = first_at_least(sizes[:-1], needed)
        runs = [shifting(cap, all_pairs) for cap in sizes]
        if halves:
            runs += [shifting(cap, upper) for cap in sizes]
            lower = jnp.sum(leaving * (devices < split)[:, None].astype(i32))
            which = which + jnp.where(lower > 0, 0, len(sizes))
        blocks = lax.switch(which, runs, blocks)
    return blocks


def plain_body(queries, keys, values, random_holder, random_offset, keep):
    tok_dev, width_dev = queries.shape
    blk_dev = tok_dev // B
    head_dev = width_dev // DH
    seq_count = lax.axis_size("seq")
    head_count = lax.axis_size("head")
    me = lax.axis_index("seq")
    count_req = blk_dev * R
    total = head_dev * count_req
    i32 = jnp.int32

    code = random_holder * blk_dev + random_offset
    code = jnp.where((keep > 0)[None, :, None], code, -1).reshape(total)
    note = jnp.concatenate([code, keep])
    note = jnp.broadcast_to(note, (seq_count * head_count,) + note.shape)
    table = lax.all_to_all(note, ("seq", "head"), split_axis=0, concat_axis=0, tiled=True)
    table = table.reshape(seq_count, head_count, total + blk_dev)
    keep_all = table[:, 0, total:].reshape(seq_count * blk_dev)
    codes = table[:, :, :total]
    devices = jnp.arange(seq_count, dtype=i32)

    halo_k, halo_v = halo(keys, "seq", B), halo(values, "seq", B)

    named = jnp.where(codes >= 0, codes // blk_dev, -1)
    counts = jnp.sum((named[..., None] == devices).astype(i32), axis=2)
    most = jnp.max(counts)
    onehot = (named[me, lax.axis_index("head")][:, None] == devices).astype(i32)
    mine = exclusive(onehot, 0)
    my_slot = jnp.sum(mine * onehot, axis=1)
    my_holder = jnp.sum(onehot * devices, axis=1)

    group = codes[:, lax.axis_index("head")]
    asks = (named[:, lax.axis_index("head")] == me).astype(i32)
    order = exclusive(asks, 1)
    full = min(total, head_dev * max(2, (count_req + seq_count - 1) // seq_count))
    chosen = asks[..., None] * (order[..., None] == jnp.arange(full, dtype=i32)).astype(i32)
    ask_head = jnp.arange(total, dtype=i32) // count_req
    ask = jnp.where(group >= 0, group % blk_dev, 0) + ask_head[None] * blk_dev
    ask = jnp.sum(chosen * ask[..., None], axis=1)
    pick_head, pick_block = ask // blk_dev, ask % blk_dev

    rank = exclusive(keep_all, 0)
    slot = rank % blk_dev
    source = jnp.arange(seq_count * blk_dev, dtype=i32) // blk_dev
    distance = jnp.where(keep_all > 0, source - rank // blk_dev, 0)
    my_slots = lax.dynamic_slice_in_dim(slot, me * blk_dev, blk_dev)
    live = jnp.stack([me > 0, me < seq_count - 1]).astype(i32)

    caps = sorted({max(1, full * part // 12) for part in range(8, 13)})

    def gathered(cap):
        def run(q, k, v, hk, hv):
            gk, gv = broadcast(jnp.stack((k[: G * B], v[: G * B])), "seq", 0)
            picked = pick(k, v, pick_head, pick_block, seq_count, cap)
            replies = lax.all_to_all(picked, "seq", split_axis=0, concat_axis=0, tiled=True)
            where = jnp.minimum(my_holder * cap + my_slot, seq_count * cap - 1)
            return attend(keep, my_slots, live, where, q, k, v, hk, hv, gk, gv, replies)

        return run

    blocks = lax.switch(
        first_at_least(caps[:-1], most),
        [gathered(cap) for cap in caps],
        queries, keys, values, halo_k, halo_v,
    )

    return settle(blocks, keep_all, slot, source, distance, me, seq_count, blk_dev)


TILE = (2 * B, DH)
SMALL = pltpu.CompilerParams(vmem_limit_bytes=60 * 1024 * 1024)


def fits(planes, tiles, most):
    slots = 2 * (planes - 1) * tiles + 2 * planes * most + most
    return slots * 2 * B * DH * 2 <= 44 * 1024 * 1024


def exchange_kernel(
    count, cz, cx, blk_dev, ztab, xtab, k_ref, v_ref,
    rand_ref, halo_ref, glob_ref, home, zs, zr, xs, own,
    z_send, z_recv, x_send, x_recv, h_send, h_recv, g_send, g_recv, l_sem,
):
    planes = count // 2
    me = lax.axis_index("seq")
    plane, side = me // 2, me % 2
    mate = plane * 2 + 1 - side
    tok = k_ref.shape[0]
    head_dev = k_ref.shape[1] // DH
    barrier = pltpu.get_barrier_semaphore()
    for step in range(1, count):
        peer = lax.rem(me + step, count)
        pl.semaphore_signal(
            barrier, inc=1, device_id={"seq": peer}, device_id_type=pl.DeviceIdType.MESH
        )
    pl.semaphore_wait(barrier, count - 1)

    def remote(src, dst, send, recv, peer):
        return pltpu.make_async_remote_copy(
            src_ref=src, dst_ref=dst, send_sem=send, recv_sem=recv,
            device_id={"seq": peer}, device_id_type=pl.DeviceIdType.MESH,
        )

    tables = (k_ref, v_ref)
    low, high = pl.ds(0, B), pl.ds(B, B)
    first, last = pl.ds(0, B), pl.ds(tok - B, B)
    after = jnp.minimum(me + 1, count - 1)
    before = jnp.maximum(me - 1, 0)
    ups = [
        remote(tables[i].at[last], halo_ref.at[i, low], h_send.at[i], h_recv.at[i], after)
        for i in range(2)
    ]
    downs = [
        remote(tables[i].at[first], halo_ref.at[i, high], h_send.at[2 + i], h_recv.at[2 + i], before)
        for i in range(2)
    ]
    local = [
        pltpu.make_async_copy(tables[i].at[pl.ds(0, G * B)], glob_ref.at[i], l_sem.at[i])
        for i in range(2)
    ]
    to_mate = [
        remote(glob_ref.at[i], glob_ref.at[i], g_send.at[i], g_recv.at[i], mate)
        for i in range(2)
    ]
    onward = [
        remote(
            glob_ref.at[i], glob_ref.at[i], g_send.at[2 + i], g_recv.at[i],
            jnp.minimum(me + 2, count - 1),
        )
        for i in range(2)
    ]

    @pl.when(me == 0)
    def _():
        for c in local:
            c.start()
        for c in local:
            c.wait()
        for c in onward:
            c.start()
        for c in to_mate:
            c.start()

    @pl.when(me < count - 1)
    def _():
        for c in ups:
            c.start()

    @pl.when(me > 0)
    def _():
        for c in downs:
            c.start()

    @pl.when(me == 0)
    def _():
        halo_ref[:, low, :] = jnp.zeros((2, B, k_ref.shape[1]), k_ref.dtype)

    @pl.when(me == count - 1)
    def _():
        halo_ref[:, high, :] = jnp.zeros((2, B, k_ref.shape[1]), k_ref.dtype)

    def load_home(block, carry):
        rows = pl.ds(pl.multiple_of(block * B, B), B)
        for h in range(head_dev):
            cols = slice(h * DH, (h + 1) * DH)
            home[h * blk_dev + block, low, :] = k_ref[rows, cols]
            home[h * blk_dev + block, high, :] = v_ref[rows, cols]
        return carry

    lax.fori_loop(0, blk_dev, load_home, 0)

    def from_slots(dst, src, table, row, cap):
        def one(j, carry):
            dst[j] = src[table[row, j]]
            return carry

        lax.fori_loop(0, cap, one, 0)

    steps = list(range(1, planes))
    steps.sort(key=lambda d: abs(d - planes / 2))
    x_base = (planes - 1) * cz
    z_copies = {
        d: remote(
            zs[d - 1], zr[d - 1], z_send.at[d - 1], z_recv.at[d - 1],
            lax.rem(plane + d, planes) * 2 + side,
        )
        for d in steps
    }
    x_copies = [
        remote(
            xs[d], rand_ref.at[pl.ds(x_base + d * cx, cx)],
            x_send.at[d], x_recv.at[d], mate,
        )
        for d in range(planes)
    ]
    for d in steps:
        from_slots(zs[d - 1], home, ztab, d - 1, cz)
        if d == steps[0]:
            continue
        z_copies[steps[steps.index(d) - 1]].start()
    from_slots(xs[0], home, xtab, 0, cx)
    z_copies[steps[-1]].start()
    from_slots(own, home, xtab, planes, cx)
    x_copies[0].start()

    @pl.when(jnp.logical_and(side == 0, plane > 0))
    def _():
        for c in to_mate:
            c.wait_recv()
        for c in to_mate:
            c.start()

        @pl.when(plane < planes - 1)
        def _():
            for c in onward:
                c.start()

    keep_own = pltpu.make_async_copy(
        own, rand_ref.at[pl.ds(x_base + planes * cx, cx)], l_sem.at[2]
    )
    keep_own.start()
    kept = []
    for d in steps:
        z_copies[d].wait_recv()
        out = pltpu.make_async_copy(
            zr[d - 1], rand_ref.at[pl.ds((d - 1) * cz, cz)], l_sem.at[2 + d]
        )
        out.start()
        kept.append(out)
        from_slots(xs[d], zr[d - 1], xtab, d, cx)
        x_copies[d].start()

    @pl.when(side == 1)
    def _():
        for c in to_mate:
            c.wait_recv()

    @pl.when(side == 0)
    def _():
        for c in to_mate:
            c.wait_send()

        @pl.when(plane < planes - 1)
        def _():
            for c in onward:
                c.wait_send()

    @pl.when(me < count - 1)
    def _():
        for c in ups:
            c.wait_send()
        for c in downs:
            c.wait_recv()

    @pl.when(me > 0)
    def _():
        for c in downs:
            c.wait_send()
        for c in ups:
            c.wait_recv()

    keep_own.wait()
    for c in kept:
        c.wait()
    for d in steps:
        z_copies[d].wait_send()
    for c in x_copies:
        c.wait()


def exchange(count, level, cz, cx, slots, blk_dev, ztab, xtab, keys, values):
    planes = count // 2
    tok, width = keys.shape
    smem = pl.BlockSpec(memory_space=pltpu.SMEM)
    vmem = pl.BlockSpec(memory_space=pltpu.VMEM)
    dtype = keys.dtype
    dma = pltpu.SemaphoreType.DMA
    return pl.pallas_call(
        functools.partial(exchange_kernel, count, cz, cx, blk_dev),
        out_shape=(
            jax.ShapeDtypeStruct((slots, *TILE), dtype),
            jax.ShapeDtypeStruct((2, 2 * B, width), dtype),
            jax.ShapeDtypeStruct((2, G * B, width), dtype),
        ),
        in_specs=[smem, smem, vmem, vmem],
        out_specs=(pl.BlockSpec(memory_space=pl.ANY), vmem, vmem),
        scratch_shapes=[
            pltpu.VMEM((tok // B * (width // DH), *TILE), dtype),
            [pltpu.VMEM((cz, *TILE), dtype) for _ in range(planes - 1)],
            [pltpu.VMEM((cz, *TILE), dtype) for _ in range(planes - 1)],
            [pltpu.VMEM((cx, *TILE), dtype) for _ in range(planes)],
            pltpu.VMEM((cx, *TILE), dtype),
            dma((planes - 1,)), dma((planes - 1,)),
            dma((planes,)), dma((planes,)),
            dma((4,)), dma((4,)), dma((4,)), dma((2,)), dma((2 + planes,)),
        ],
        compiler_params=pltpu.CompilerParams(
            collective_id=level, has_side_effects=True,
            vmem_limit_bytes=60 * 1024 * 1024,
        ),
    )(ztab, xtab, keys, values)


CHUNK = 8


def near_far_kernel(
    blk_dev, keep_ref, slot_ref, live_ref, where_ref, used_ref,
    q_ref, k_ref, v_ref, hk_ref, hv_ref, gk_ref, gv_ref, rand_hbm, out_ref, rand_ref, sems,
):
    scale = 1.0 / math.sqrt(DH)
    head = pl.program_id(0)
    chunks = rand_hbm.shape[0] // CHUNK

    @pl.when(head == 0)
    def _():
        def copy(c):
            rows = pl.ds(c * CHUNK, CHUNK)
            return pltpu.make_async_copy(rand_hbm.at[rows], rand_ref.at[rows], sems.at[c])

        for c in range(chunks):
            pl.when(c * CHUNK < used_ref[0])(lambda c=c: copy(c).start())
        for c in range(chunks):
            pl.when(c * CHUNK < used_ref[0])(lambda c=c: copy(c).wait())

    out_ref[...] = jnp.zeros_like(out_ref)

    def tile(ref, halo_ref, i):
        if i < 0:
            return halo_ref[0, :B]
        if i >= blk_dev:
            return halo_ref[0, B:]
        return ref[i * B : (i + 1) * B]

    def one(i):
        q = q_ref[i * B : (i + 1) * B]
        near = range(i - 1, i + 2)
        picks = [where_ref[(head * blk_dev + i) * R + r] for r in range(R)]
        k_parts = [
            jnp.concatenate([tile(k_ref, hk_ref, n) for n in near], axis=0),
            gk_ref[0],
            jnp.concatenate([rand_ref[p, :B] for p in picks], axis=0),
        ]
        v_parts = [
            jnp.concatenate([tile(v_ref, hv_ref, n) for n in near], axis=0),
            gv_ref[0],
            jnp.concatenate([rand_ref[p, B:] for p in picks], axis=0),
        ]
        scores = [
            lax.dot_general(
                q, k, (((1,), (1,)), ((), ())), preferred_element_type=jnp.float32
            )
            * scale
            for k in k_parts
        ]
        lanes = lax.broadcasted_iota(jnp.int32, scores[0].shape, 1)
        if i == 0:
            dead = jnp.logical_and(lanes < B, live_ref[0] == 0)
            scores[0] = jnp.where(dead, neg_big, scores[0])
        if i == blk_dev - 1:
            dead = jnp.logical_and(lanes >= 2 * B, live_ref[1] == 0)
            scores[0] = jnp.where(dead, neg_big, scores[0])
        peak = functools.reduce(
            jnp.maximum, [jnp.max(s, axis=-1, keepdims=True) for s in scores]
        )
        numer = jnp.zeros((B, DH), jnp.float32)
        denom = jnp.zeros((B, 1), jnp.float32)
        for s, v in zip(scores, v_parts):
            w = jnp.exp(s - peak).astype(jnp.bfloat16)
            denom = denom + jnp.sum(w.astype(jnp.float32), axis=-1, keepdims=True)
            numer = numer + jnp.dot(w, v, preferred_element_type=jnp.float32)
        rows = pl.ds(pl.multiple_of(slot_ref[i] * B, B), B)
        out_ref[rows, :] = (numer / denom).astype(out_ref.dtype)

    for i in range(blk_dev):
        pl.when(keep_ref[i] > 0)(functools.partial(one, i))


def near_far(keep, slot, live, where, used, q, k, v, halo_kv, glob, rand):
    tok_dev, width_dev = q.shape
    blk_dev, head_dev = tok_dev // B, width_dev // DH

    def column(rows):
        return pl.BlockSpec((rows, DH), lambda h, *_: (0, h))

    def part(rows, which):
        return pl.BlockSpec((1, rows, DH), lambda h, *_: (which, 0, h))

    return pl.pallas_call(
        functools.partial(near_far_kernel, blk_dev),
        out_shape=jax.ShapeDtypeStruct(q.shape, q.dtype),
        grid_spec=pltpu.PrefetchScalarGridSpec(
            num_scalar_prefetch=5,
            grid=(head_dev,),
            in_specs=[column(tok_dev)] * 3
            + [part(2 * B, 0), part(2 * B, 1), part(G * B, 0), part(G * B, 1)]
            + [pl.BlockSpec(memory_space=pl.ANY)],
            out_specs=column(tok_dev),
            scratch_shapes=[
                pltpu.VMEM(rand.shape, rand.dtype),
                pltpu.SemaphoreType.DMA((rand.shape[0] // CHUNK,)),
            ],
        ),
        compiler_params=ANYWHERE,
    )(keep, slot, live, where, used, q, k, v, halo_kv, halo_kv, glob, glob, rand)


def levels(tiles, most):
    caps = []
    for part in (22, 24, 26, 28, 30, 32, 36):
        cz = min(tiles, tiles * part // 64)
        caps.append((cz, min(most, max(1, most * (part // 2 + 4) // 24))))
    caps.append((tiles, most))
    return sorted(set(caps))


def body(queries, keys, values, random_holder, random_offset, keep):
    tok_dev, width_dev = queries.shape
    blk_dev = tok_dev // B
    head_dev = width_dev // DH
    count = lax.axis_size("seq")
    head_count = lax.axis_size("head")
    count_req = blk_dev * R
    total = head_dev * count_req
    tiles = head_dev * blk_dev
    most = min(tiles, head_dev * max(2, (count_req + count - 1) // count))
    planes = count // 2
    if count % 2 or planes < 2 or not fits(planes, tiles, most):
        return plain_body(queries, keys, values, random_holder, random_offset, keep)
    me = lax.axis_index("seq")
    plane, side = me // 2, me % 2
    mate = me + 1 - 2 * side
    i32, f32 = jnp.int32, jnp.float32

    code = random_holder * blk_dev + random_offset
    code = jnp.where((keep > 0)[None, :, None], code, -1).reshape(total)
    note = jnp.concatenate([code, keep])
    note = jnp.broadcast_to(note, (count * head_count,) + note.shape)
    table = lax.all_to_all(note, ("seq", "head"), split_axis=0, concat_axis=0, tiled=True)
    table = table.reshape(count, head_count, total + blk_dev)
    keep_all = table[:, 0, total:].reshape(count * blk_dev)
    codes = table[:, :, :total].reshape(count, head_count, head_dev, 1, count_req)

    blocks = jnp.arange(count * blk_dev, dtype=i32)[:, None]
    need = jnp.max((codes == blocks).astype(i32), axis=-1)
    need = need.reshape(count, head_count, head_dev, count, blk_dev)
    both = jnp.max(need.reshape(planes, 2, *need.shape[1:]), axis=1)
    devices = jnp.arange(count, dtype=i32)
    away = (devices[None] // 2 != jnp.arange(planes, dtype=i32)[:, None]).astype(i32)
    most_z = jnp.max(jnp.sum(both, axis=(2, 4)) * away[:, None])
    most_x = jnp.max(jnp.sum(need, axis=(2, 4)))

    group = lax.axis_index("head")

    def flat(array):
        array = lax.dynamic_index_in_dim(array, group, 1, keepdims=False)
        return jnp.transpose(array, (0, 2, 1, 3)).reshape(array.shape[0], count, tiles)

    want, want_z = flat(need), flat(both)
    order = jnp.arange(tiles, dtype=i32)
    before = (order[:, None] < order[None]).astype(f32)

    def places(flags):
        got = jnp.dot(flags.astype(jnp.bfloat16), before.astype(jnp.bfloat16), preferred_element_type=f32)
        return got.astype(i32)

    slot_x, slot_z = places(want), places(want_z)

    def listed(flags, slots, worth, cap):
        hit = flags[:, None] * (slots[:, None] == jnp.arange(cap, dtype=i32)[:, None]).astype(i32)
        return jnp.sum(hit * worth[:, None], axis=2)

    def at(array, i):
        return lax.dynamic_index_in_dim(array, i, 0, keepdims=False)

    steps = jnp.arange(planes, dtype=i32)
    goal = (plane + steps[1:]) % planes
    mine_z, mine_slot_z = jnp.take(want_z[:, me], goal, axis=0), jnp.take(slot_z[:, me], goal, axis=0)
    plain = jnp.broadcast_to(order, (planes + 1, tiles))
    ztab = listed(mine_z, mine_slot_z, plain[: planes - 1], tiles)
    here = at(slot_z, plane)
    source = ((plane - steps) % planes) * 2 + side
    worth = jnp.where((steps == 0)[:, None], order, jnp.take(here, source, axis=0))
    asked = jnp.concatenate([jnp.take(at(want, mate), source, axis=0), at(want, me)[me][None]])
    asked_slot = jnp.concatenate([jnp.take(at(slot_x, mate), source, axis=0), at(slot_x, me)[me][None]])
    xtab = listed(asked, asked_slot, jnp.concatenate([worth, order[None]]), most)

    caps = levels(tiles, most)
    cz_of = jnp.asarray([c[0] for c in caps], i32)
    cx_of = jnp.asarray([c[1] for c in caps], i32)
    level = jnp.sum(((most_z > cz_of) | (most_x > cx_of))[:-1].astype(i32))
    cz, cx = cz_of[level], cx_of[level]
    gap = (plane - devices // 2) % planes
    x_base = (planes - 1) * cz
    straight = jnp.where(devices == me, x_base + planes * cx, (gap - 1) * cz)
    start = jnp.where(devices % 2 == side, straight, x_base + gap * cx)
    by_z = ((devices % 2 == side) & (devices != me))[:, None]
    spot = start[:, None] + jnp.where(by_z, here, at(slot_x, me))
    spot = jnp.transpose(spot.reshape(count, head_dev, blk_dev), (1, 0, 2)).reshape(head_dev, 1, count * blk_dev)
    picks = (random_holder * blk_dev + random_offset).reshape(head_dev, count_req, 1)
    hits = (picks == jnp.arange(count * blk_dev, dtype=i32)).astype(i32)
    where = jnp.sum(hits * spot, axis=2).reshape(total)
    used = x_base + (planes + 1) * cx

    slots_all = -(-max((planes - 1) * c[0] + (planes + 1) * c[1] for c in caps) // CHUNK) * CHUNK
    where = jnp.minimum(where, slots_all - 1)

    def exchanged(number, caps):
        def run(ztab, xtab, k, v):
            return exchange(count, number, *caps, slots_all, blk_dev, ztab, xtab, k, v)

        return run

    rand, halo_kv, glob = lax.switch(
        level, [exchanged(n, c) for n, c in enumerate(caps)], ztab, xtab, keys, values
    )

    rank = exclusive(keep_all, 0)
    slot = rank % blk_dev
    source = jnp.arange(count * blk_dev, dtype=i32) // blk_dev
    distance = jnp.where(keep_all > 0, source - rank // blk_dev, 0)
    my_slots = lax.dynamic_slice_in_dim(slot, me * blk_dev, blk_dev)
    live = jnp.stack([me > 0, me < count - 1]).astype(i32)
    blocks = near_far(
        keep, my_slots, live, where, used[None], queries, keys, values, halo_kv, glob, rand
    )
    return settle(blocks, keep_all, slot, source, distance, me, count, blk_dev)


def solution(mesh):
    in_specs = (
        P("seq", "head"),
        P("seq", "head"),
        P("seq", "head"),
        P("head", "seq", None),
        P("head", "seq", None),
        P("seq"),
    )
    out_specs = P("seq", "head")
    return jax.shard_map(body, mesh=mesh, in_specs=in_specs, out_specs=out_specs, check_vma=False)
```

profile of v0, /device:TPU:10, one launch (start us, length us, event | category | flops | bytes accessed | tf_op | source)
XLA Modules:
  0.0 539.4 jit_solution(2260432367772176747)
XLA Ops:
  0.0 0.7 broadcast_compare_fusion
  0.7 0.7 broadcast_select_fusion.8
  1.7 0.7 pad_add_fusion.3
  2.4 0.6 broadcast_in_dim.84
  3.0 6.0 %all-to-all-start = ((s32[32,1,200]{2,1,0:T(1,128)}), s32[32,1,200]{2,1,0:T(1,128)S(1)}, u32[]{:S(2)}, u32[]{:S(2)}) async-start(s32[32,1,200]{2,1,0:T(1,128)} %broadcast_in_dim.84), calls=%async_computation | async-start | bytes 65536 | tf_op jit(solution)/shard_map/all_to_all | solution.py:701
  9.3 0.6 add_convert_fusion.live_ref
  10.1 4.2 all-to-all-done
  14.5 1.4 convert_reduce_fusion
  16.3 1.3 reshape.540
  17.7 0.6 reduce_sum.232
  18.5 0.6 reduce_max.69
  19.5 0.7 fusion.92
  20.2 1.2 compare_or_fusion
  21.4 0.7 fusion.108
  24.1 0.6 dynamic_slice.207
  24.7 0.6 dynamic_slice.206
  27.3 0.4 multiply_reduce_fusion.12
  27.8 0.6 reduce_max.65
  28.5 0.4 multiply_reduce_fusion.14
  28.9 0.7 reduce_max.63
  29.6 0.7 reduce_max.64
  30.4 0.7 multiply_reduce_fusion.16
  32.9 2.6 fusion.107
  36.7 0.7 dynamic_slice.205.slot_ref
  37.4 1.0 dynamic-slice_bitcast_fusion
  39.4 1.1 compare_select_fusion.48
  41.0 0.6 min.89.where_ref
  41.7 0.6 gather_fusion
  42.2 0.6 gather_fusion.1
  42.8 0.6 gather_fusion.2
  43.3 0.6 gather_fusion.3
  43.9 0.6 gather_fusion.4
  45.7 215.2 %conditional.4 = ((bf16[312,256,128]{2,1,0:T(8,128)(2,1)}, bf16[2,256,1024]{2,1,0:T(8,128)(2,1)S(1)}, bf16[2,256,1024]{2,1,0:T(8,128)(2,1)})) conditional(s32[]{:T(128)} %clamp.27, (s32[3,64]{1,0:T(4,128)S(1)}, s32[5,24]{1,0:T(8,128)S(1)}, bf16[1024,1024]{1,0:T(8,128)(2,1)S(1)}, ...), branch_computations={%region_23.26_spmd, %region_24.27_spmd, %region_25.28_spmd, %regio... | conditional | bytes 8 | solution.py:776
  45.7 215.0 %branch_4_fun.7 = (bf16[312,256,128]{2,1,0:T(8,128)(2,1)}, bf16[2,256,1024]{2,1,0:T(8,128)(2,1)S(1)}, bf16[2,256,1024]{2,1,0:T(8,128)(2,1)}) custom-call(s32[3,64]{1,0:T(4,128)S(1)} %get-tuple-element.762.ztab, s32[5,24]{1,0:T(8,128)S(1)} %get-tuple-element.763.xtab, bf16[1024,1024]{1,0:T(8,128)(2,1)S(1)} %get-tuple-element.764.k_ref, ...), custom_call_target="tpu_custom_call" | custom-call | tf_op jit(solution)/shard_map/cond/branch_4_fun/pallas_call | solution.py:540
  260.9 22.0 %shard_map.119 = bf16[1024,1024]{1,0:T(8,128)(2,1)S(1)} custom-call(s32[8]{0:T(128)} %keep_ref.1, s32[8]{0:T(128)} %dynamic_slice.205.slot_ref, s32[2]{0:T(128)} %add_convert_fusion.live_ref, s32[192]{0:T(256)} %min.89.where_ref, s32[1]{0:T(128)} %bitcast.58.used_ref, bf16[1024,1024]{1,0:T(8,128)(2,1)} %q_ref.1, bf16[1024,1024]{1,0:T(8,128)(2,1)} %k_ref.1, ...), custom_call_target="tpu_custom_call" | custom-call | tf_op jit(solution)/shard_map/pallas_call | solution.py:651
  283.0 133.7 %conditional.5 = (bf16[1024,1024]{1,0:T(8,128)(2,1)S(1)}) conditional(s32[]{:T(128)} %clamp.26, bf16[1024,1024]{1,0:T(8,128)(2,1)S(1)} %shard_map.119, (pred[8]{0:T(512)(128)(4,1)S(1)}, s32[8,8]{1,0:T(8,128)S(1)}, bf16[1024,1024]{1,0:T(8,128)(2,1)S(1)}, pred[8]{0:T(512)(128)(4,1)S(1)}, s32[8,8]{1,0:T(8,128)S(1)}, ...), branch_computations={%region_34.37_spmd, %region_35.38_spmd, %region_36.39_spmd, %regio... | conditional | flops 352 | bytes 20973544 | solution.py:259
  283.0 1.3 copy.125.in_ref.old_ref
  284.3 0.6 fusion.52.order_ref
  285.0 3.8 branch_2_fun.8
  288.8 11.2 %collective-permute-start.2 = (bf16[640,1024]{1,0:T(8,128)(2,1)}, bf16[640,1024]{1,0:T(8,128)(2,1)S(1)}, u32[]{:S(2)}, u32[]{:S(2)}) collective-permute-start(bf16[640,1024]{1,0:T(8,128)(2,1)} %branch_2_fun.8), channel_id=1, source_target_pairs={{4,0},{8,4},{12,8},{16,12},{20,16},{24,20},{28,24},{5,1},{9,5},{13... | collective-permute-start | bytes 3932168 | tf_op jit(solution)/shard_map/cond/branch_2_fun/ppermute | solution.py:248
  299.9 0.6 fusion.55
  300.5 110.3 %collective-permute-done.2.new_ref = bf16[640,1024]{1,0:T(8,128)(2,1)S(1)} collective-permute-done((bf16[640,1024]{1,0:T(8,128)(2,1)}, bf16[640,1024]{1,0:T(8,128)(2,1)S(1)}, u32[]{:S(2)}, u32[]{:S(2)}) %collective-permute-start.2) | collective-permute-done | bytes 1310752 | tf_op jit(solution)/shard_map/cond/branch_2_fun/ppermute | solution.py:248
  410.8 1.1 copy-done.10
  411.8 4.8 branch_2_fun.9
  416.7 83.9 %conditional.6 = (bf16[1024,1024]{1,0:T(8,128)(2,1)S(1)}) conditional(s32[]{:T(128)} %clamp.25, bf16[1024,1024]{1,0:T(8,128)(2,1)S(1)} %get-tuple-element.1303, (pred[8]{0:T(512)(128)(4,1)S(1)}, s32[8,8]{1,0:T(8,128)S(1)}, bf16[1024,1024]{1,0:T(8,128)(2,1)S(1)}, pred[8]{0:T(512)(128)(4,1)S(1)}, s32[8,8]{1,0:T(8,128)S(1)}, ...), branch_computations={%region_42.45_spmd, %region_43.46_spmd, %region_44.47_spmd, %regio... | conditional | flops 352 | bytes 20973544 | solution.py:259
  416.8 1.3 copy.131.in_ref.old_ref
  418.1 0.6 fusion.82.order_ref
  418.7 5.5 %branch_4_fun.10 = bf16[1024,1024]{1,0:T(8,128)(2,1)} custom-call(s32[8]{0:T(128)} %fusion.82.order_ref, bf16[1024,1024]{1,0:T(8,128)(2,1)} %copy.131.in_ref.old_ref), custom_call_target="tpu_custom_call" | custom-call | tf_op jit(solution)/shard_map/cond/branch_4_fun/pallas_call | solution.py:162
  424.2 1.9 collective-permute-start.7
  426.1 0.6 fusion.85
  426.7 67.6 %collective-permute-done.7.new_ref = bf16[1024,1024]{1,0:T(8,128)(2,1)S(1)} collective-permute-done((bf16[1024,1024]{1,0:T(8,128)(2,1)}, bf16[1024,1024]{1,0:T(8,128)(2,1)S(1)}, u32[]{:S(2)}, u32[]{:S(2)}) %collective-permute-start.7) | collective-permute-done | bytes 2097184 | tf_op jit(solution)/shard_map/cond/branch_4_fun/ppermute | solution.py:248
  494.3 1.3 copy-done.3
  495.6 5.0 branch_4_fun.11
  500.7 37.4 %conditional.7 = (bf16[1024,1024]{1,0:T(8,128)(2,1)S(1)}) conditional(s32[]{:T(128)} %clamp.24, bf16[1024,1024]{1,0:T(8,128)(2,1)S(1)} %get-tuple-element.1304, (s32[]{:T(128)}, s32[8,8]{1,0:T(8,128)S(1)}, s32[8]{0:T(128)S(1)}, s32[]{:T(128)}, s32[8]{0:T(128)S(1)}, /*index=5*/s32[8]{0:T(128)S(1)}, ...), branch_computations={%region_48.51_spmd, %region_49.53_spmd, %region_51.55_spmd, %regio... | conditional | flops 382 | bytes 20973724 | solution.py:259
  500.7 1.3 copy.136.in_ref.old_ref
  502.1 0.6 fusion.36
  502.7 0.5 compare_select_fusion.16
  503.2 0.6 multiply_reduce_fusion.4.order_ref
  503.8 3.2 branch_6_fun.4
  507.0 1.3 collective-permute-start.12
  508.3 23.8 %collective-permute-done.12.new_ref = bf16[512,1024]{1,0:T(8,128)(2,1)S(1)} collective-permute-done((bf16[512,1024]{1,0:T(8,128)(2,1)}, bf16[512,1024]{1,0:T(8,128)(2,1)S(1)}, u32[]{:S(2)}, u32[]{:S(2)}) %collective-permute-start.12) | collective-permute-done | bytes 1048608 | tf_op jit(solution)/shard_map/cond/branch_6_fun/ppermute | solution.py:248
  532.1 1.0 copy-done.17
  533.1 5.0 branch_6_fun.5
  538.1 1.3 copy-done
  (102 shorter events, 4.9 us)
Async XLA Ops:
  3.0 11.2 %all-to-all-start = ((s32[32,1,200]{2,1,0:T(1,128)}), s32[32,1,200]{2,1,0:T(1,128)S(1)}, u32[]{:S(2)}, u32[]{:S(2)}) async-start(s32[32,1,200]{2,1,0:T(1,128)} %broadcast_in_dim.84), calls=%async_computation | async-start | bytes 65536 | tf_op jit(solution)/shard_map/all_to_all | solution.py:701
  10.1 8.4 %copy-start.18 = (s32[5,64]{1,0:T(8,128)}, s32[5,64]{1,0:T(8,128)S(1)}, u32[]{:S(2)}) copy-start(s32[5,64]{1,0:T(8,128)S(1)} %broadcast_in_dim.88) | copy-start | bytes 3844
  16.3 3.9 copy-start.20
  16.3 3.9 copy-start.21
  17.6 15.3 %copy-start.19 = (s32[4]{0:T(128)S(1)}, s32[4]{0:T(128)}, u32[]{:S(2)}) copy-start(s32[4]{0:T(128)} %constant.413.clone) | copy-start | bytes 52
  18.5 27.1 %copy-start.1 = (bf16[1024,1024]{1,0:T(8,128)(2,1)S(1)}, bf16[1024,1024]{1,0:T(8,128)(2,1)}, u32[]{:S(2)}) copy-start(bf16[1024,1024]{1,0:T(8,128)(2,1)} %k_ref.1) | copy-start | bytes 6291460
  19.2 26.1 %slice-start = ((s32[5,64]{1,0:T(8,128)}), s32[3,64]{1,0:T(4,128)S(1)}, s32[]{:S(2)}) async-start(s32[5,64]{1,0:T(8,128)} %copy-done.18), calls=%async_computation.1 | async-start | bytes 4096 | tf_op jit(solution)/shard_map/slice | solution.py:742
  288.8 122.0 %collective-permute-start.2 = (bf16[640,1024]{1,0:T(8,128)(2,1)}, bf16[640,1024]{1,0:T(8,128)(2,1)S(1)}, u32[]{:S(2)}, u32[]{:S(2)}) collective-permute-start(bf16[640,1024]{1,0:T(8,128)(2,1)} %branch_2_fun.8), channel_id=1, source_target_pairs={{4,0},{8,4},{12,8},{16,12},{20,16},{24,20},{28,24},{5,1},{9,5},{13... | collective-permute-start | bytes 3932168 | tf_op jit(solution)/shard_map/cond/branch_2_fun/ppermute | solution.py:248
  410.8 1.1 copy-start.10
  424.2 70.1 %collective-permute-start.7 = (bf16[1024,1024]{1,0:T(8,128)(2,1)}, bf16[1024,1024]{1,0:T(8,128)(2,1)S(1)}, u32[]{:S(2)}, u32[]{:S(2)}) collective-permute-start(bf16[1024,1024]{1,0:T(8,128)(2,1)} %branch_4_fun.10), channel_id=1, source_target_pairs={{8,0},{12,4},{16,8},{20,12},{24,16},{28,20},{9,1},{13,5},{17,9},{2... | collective-permute-start | bytes 6291464 | tf_op jit(solution)/shard_map/cond/branch_4_fun/ppermute | solution.py:248
  494.3 1.4 copy-start.3
  507.0 25.1 %collective-permute-start.12 = (bf16[512,1024]{1,0:T(8,128)(2,1)}, bf16[512,1024]{1,0:T(8,128)(2,1)S(1)}, u32[]{:S(2)}, u32[]{:S(2)}) collective-permute-start(bf16[512,1024]{1,0:T(8,128)(2,1)} %branch_6_fun.4), channel_id=1, source_target_pairs={{24,8},{28,12},{25,9},{29,13},{26,10},{30,14},{27,11},{31,15}} | collective-permute-start | bytes 3145736 | tf_op jit(solution)/shard_map/cond/branch_6_fun/ppermute | solution.py:248
  532.1 1.0 copy-start.17
  538.1 1.3 copy-start
where the time goes:
time: 545 us; the launch traced here: 539 us
  Pallas kernels  264 us (48%)
  waiting for transfers between devices  206 us (38%)
  other arithmetic  22 us (4%)
  starting transfers between devices  20.4 us (4%)
  local copies, waits for them, and re-layouts  18.7 us (3%)
  between operations  7.47 us (1%)
    pallas_call x1, Pallas kernels, exchange(): pl.pallas_call(functools.partial(exchange_kernel, count, cz, cx, blk_dev)...  215 us
    ppermute x3, waiting for transfers between devices, run(): moved = lax.ppermute(take_blocks(blocks, send, cap), 'seq', pairs)  202 us
    pallas_call x1, Pallas kernels, near_far(): pl.pallas_call(functools.partial(near_far_kernel, blk_dev), out_shape=jax...  22 us
    pallas_call x3, Pallas kernels, merge_blocks(): pl.pallas_call(merge_kernel, out_shape=jax.ShapeDtypeStruct(old.shape, ol...  14.9 us
    ppermute x3, starting transfers between devices, run(): moved = lax.ppermute(take_blocks(blocks, send, cap), 'seq', pairs)  14.4 us
    pallas_call x3, Pallas kernels, take_blocks(): pl.pallas_call(copy_kernel, out_shape=jax.ShapeDtypeStruct((cap * B, widt...  12.4 us
  transfers between devices with their start and end apart: 4, of which 4 were waited for; matrix products, arithmetic and copies ran while one was open for 0% of the time, Pallas kernels for 0%

commit v1 on v0

--- a/solution.py
+++ b/solution.py
@@ -380,17 +380,10 @@
         pltpu.make_async_copy(tables[i].at[pl.ds(0, G * B)], glob_ref.at[i], l_sem.at[i])
         for i in range(2)
     ]
-    to_mate = [
-        remote(glob_ref.at[i], glob_ref.at[i], g_send.at[i], g_recv.at[i], mate)
-        for i in range(2)
-    ]
-    onward = [
-        remote(
-            glob_ref.at[i], glob_ref.at[i], g_send.at[2 + i], g_recv.at[i],
-            jnp.minimum(me + 2, count - 1),
-        )
-        for i in range(2)
-    ]
+    item = glob_ref.at[side]
+    chain = remote(item, item, g_send.at[0], g_recv.at[0], jnp.minimum(me + 2, count - 1))
+    swap = remote(item, item, g_send.at[1], g_recv.at[1], mate)
+    extra = remote(glob_ref.at[1], glob_ref.at[1], g_send.at[2], g_recv.at[0], mate)
 
     @pl.when(me == 0)
     def _():
@@ -398,10 +391,22 @@
             c.start()
         for c in local:
             c.wait()
-        for c in onward:
-            c.start()
-        for c in to_mate:
-            c.start()
+        chain.start()
+        extra.start()
+        swap.start()
+
+    def pass_on():
+        @pl.when(me > 0)
+        def _():
+            chain.wait_recv()
+
+            @pl.when(plane < planes - 1)
+            def _():
+                chain.start()
+
+            @pl.when(me > 1)
+            def _():
+                swap.start()
 
     @pl.when(me < count - 1)
     def _():
@@ -438,15 +443,17 @@
 
         lax.fori_loop(0, cap, one, 0)
 
-    steps = list(range(1, planes))
-    steps.sort(key=lambda d: abs(d - planes / 2))
+    half = planes // 2
+    lower = plane < half
+    rest = [d for d in range(1, planes) if d != half]
+    rising, falling = [half, *rest], [half, *reversed(rest)]
     x_base = (planes - 1) * cz
     z_copies = {
         d: remote(
             zs[d - 1], zr[d - 1], z_send.at[d - 1], z_recv.at[d - 1],
             lax.rem(plane + d, planes) * 2 + side,
         )
-        for d in steps
+        for d in rising
     }
     x_copies = [
         remote(
@@ -455,57 +462,68 @@
         )
         for d in range(planes)
     ]
-    for d in steps:
+    from_slots(zs[half - 1], home, ztab, half - 1, cz)
+    from_slots(xs[0], home, xtab, 0, cx)
+    z_copies[half].start()
+    for d in rest:
         from_slots(zs[d - 1], home, ztab, d - 1, cz)
-        if d == steps[0]:
-            continue
-        z_copies[steps[steps.index(d) - 1]].start()
-    from_slots(xs[0], home, xtab, 0, cx)
-    z_copies[steps[-1]].start()
+    x_copies[0].start()
+
+    @pl.when(lower)
+    def _():
+        pass_on()
+        for d in falling[1:]:
+            z_copies[d].start()
+
+    @pl.when(jnp.logical_not(lower))
+    def _():
+        for d in rising[1:]:
+            z_copies[d].start()
+        pass_on()
+
     from_slots(own, home, xtab, planes, cx)
-    x_copies[0].start()
-
-    @pl.when(jnp.logical_and(side == 0, plane > 0))
-    def _():
-        for c in to_mate:
-            c.wait_recv()
-        for c in to_mate:
-            c.start()
-
-        @pl.when(plane < planes - 1)
-        def _():
-            for c in onward:
-                c.start()
-
     keep_own = pltpu.make_async_copy(
         own, rand_ref.at[pl.ds(x_base + planes * cx, cx)], l_sem.at[2]
     )
     keep_own.start()
-    kept = []
-    for d in steps:
-        z_copies[d].wait_recv()
-        out = pltpu.make_async_copy(
+    outs = {
+        d: pltpu.make_async_copy(
             zr[d - 1], rand_ref.at[pl.ds((d - 1) * cz, cz)], l_sem.at[2 + d]
         )
-        out.start()
-        kept.append(out)
+        for d in rising
+    }
+
+    def forward(d):
+        z_copies[d].wait_recv()
+        outs[d].start()
         from_slots(xs[d], zr[d - 1], xtab, d, cx)
         x_copies[d].start()
 
-    @pl.when(side == 1)
-    def _():
-        for c in to_mate:
-            c.wait_recv()
-
-    @pl.when(side == 0)
-    def _():
-        for c in to_mate:
-            c.wait_send()
-
-        @pl.when(plane < planes - 1)
-        def _():
-            for c in onward:
-                c.wait_send()
+    @pl.when(lower)
+    def _():
+        for d in falling:
+            forward(d)
+
+    @pl.when(jnp.logical_not(lower))
+    def _():
+        for d in rising:
+            forward(d)
+
+    @pl.when(me > 0)
+    def _():
+        swap.wait_recv()
+
+    @pl.when(plane < planes - 1)
+    def _():
+        chain.wait_send()
+
+    @pl.when(me == 0)
+    def _():
+        extra.wait_send()
+
+    @pl.when(me != 1)
+    def _():
+        swap.wait_send()
 
     @pl.when(me < count - 1)
     def _():
@@ -522,9 +540,8 @@
             c.wait_recv()
 
     keep_own.wait()
-    for c in kept:
-        c.wait()
-    for d in steps:
+    for d in rising:
+        outs[d].wait()
         z_copies[d].wait_send()
     for c in x_copies:
         c.wait()
@@ -554,7 +571,7 @@
             pltpu.VMEM((cx, *TILE), dtype),
             dma((planes - 1,)), dma((planes - 1,)),
             dma((planes,)), dma((planes,)),
-            dma((4,)), dma((4,)), dma((4,)), dma((2,)), dma((2 + planes,)),
+            dma((4,)), dma((4,)), dma((3,)), dma((2,)), dma((2 + planes,)),
         ],
         compiler_params=pltpu.CompilerParams(
             collective_id=level, has_side_effects=True,
@@ -563,11 +580,203 @@
     )(ztab, xtab, keys, values)
 
 
+PIECES = 4
+
+
+def settle_kernel(
+    count, caps, cx, blk_dev, ztab, xtab, otab, in_ref, out_ref,
+    mine, zs, pool, xs, xr, z_send, z_recv, x_send, x_recv,
+):
+    planes = count // 2
+    me = lax.axis_index("seq")
+    plane, side = me // 2, me % 2
+    mate = plane * 2 + 1 - side
+    wide = in_ref.shape[1] // PIECES
+    barrier = pltpu.get_barrier_semaphore()
+    for step in range(1, count):
+        peer = lax.rem(me + step, count)
+        pl.semaphore_signal(
+            barrier, inc=1, device_id={"seq": peer}, device_id_type=pl.DeviceIdType.MESH
+        )
+    pl.semaphore_wait(barrier, count - 1)
+
+    def remote(src, dst, send, recv, peer):
+        return pltpu.make_async_remote_copy(
+            src_ref=src, dst_ref=dst, send_sem=send, recv_sem=recv,
+            device_id={"seq": peer}, device_id_type=pl.DeviceIdType.MESH,
+        )
+
+    used = [d for d in range(1, planes) if caps[d - 1] > 0]
+    used.sort(reverse=True)
+    base = {d: blk_dev + sum(caps[: d - 1]) for d in used}
+
+    def fill(dst, src, table, row, cap):
+        def one(j, carry):
+            dst[j] = src[table[row, j]]
+            return carry
+
+        lax.fori_loop(0, cap, one, 0)
+
+    def own_part(piece):
+        def one(j, carry):
+            rows = pl.ds(pl.multiple_of(j * B, B), B)
+            block = in_ref[rows, piece * wide : (piece + 1) * wide]
+            mine[piece][j] = block
+            pool[piece][j] = block
+            return carry
+
+        lax.fori_loop(0, blk_dev, one, 0)
+
+    z_copies, x_copies = {}, []
+    for piece in range(PIECES):
+        for n, d in enumerate(used):
+            z_copies[piece, d] = remote(
+                zs[piece][n], pool[piece].at[pl.ds(base[d], caps[d - 1])],
+                z_send.at[piece, n], z_recv.at[piece, n],
+                jnp.maximum(me - 2 * d, 0),
+            )
+        x_copies.append(remote(xs[piece], xr[piece], x_send.at[piece], x_recv.at[piece], mate))
+    def start_z(piece):
+        for d in used:
+            @pl.when(plane >= d)
+            def _(d=d):
+                z_copies[piece, d].start()
+
+    for piece in range(PIECES):
+        own_part(piece)
+        for n, d in enumerate(used):
+            fill(zs[piece][n], mine[piece], ztab, d - 1, caps[d - 1])
+        if piece > 0:
+            start_z(piece - 1)
+    start_z(PIECES - 1)
+
+    def finish(piece):
+        x_copies[piece].wait_recv()
+
+        def one(j, carry):
+            rows = pl.ds(pl.multiple_of(j * B, B), B)
+            kind = otab[0, j]
+            near, far = pool[piece][otab[1, j]], xr[piece][otab[2, j]]
+            block = jnp.where(kind == 1, near, jnp.where(kind == 2, far, jnp.zeros_like(far)))
+            out_ref[rows, piece * wide : (piece + 1) * wide] = block
+            return carry
+
+        lax.fori_loop(0, blk_dev, one, 0)
+
+    for piece in range(PIECES):
+        for d in used:
+            @pl.when(plane + d < planes)
+            def _(d=d, piece=piece):
+                z_copies[piece, d].wait_recv()
+        fill(xs[piece], pool[piece], xtab, 0, cx)
+        x_copies[piece].start()
+        if piece > 0:
+            finish(piece - 1)
+    finish(PIECES - 1)
+    for piece in range(PIECES):
+        x_copies[piece].wait_send()
+        for d in used:
+            @pl.when(plane >= d)
+            def _(d=d, piece=piece):
+                z_copies[piece, d].wait_send()
+
+
+def settled(count, number, caps, cx, blk_dev, ztab, xtab, otab, blocks):
+    tok, width = blocks.shape
+    planes, wide = count // 2, width // PIECES
+    smem = pl.BlockSpec(memory_space=pltpu.SMEM)
+    vmem = pl.BlockSpec(memory_space=pltpu.VMEM)
+    dma, dtype = pltpu.SemaphoreType.DMA, blocks.dtype
+    sent = [caps[d - 1] for d in range(planes - 1, 0, -1) if caps[d - 1] > 0]
+
+    def each(rows):
+        return [pltpu.VMEM((rows, B, wide), dtype) for _ in range(PIECES)]
+
+    return pl.pallas_call(
+        functools.partial(settle_kernel, count, caps, cx, blk_dev),
+        out_shape=jax.ShapeDtypeStruct(blocks.shape, dtype),
+        in_specs=[smem, smem, smem, vmem],
+        out_specs=vmem,
+        scratch_shapes=[
+            each(blk_dev),
+            [[pltpu.VMEM((c, B, wide), dtype) for c in sent] for _ in range(PIECES)],
+            each(blk_dev + sum(caps)),
+            each(cx),
+            each(cx),
+            dma((PIECES, len(sent))), dma((PIECES, len(sent))), dma((PIECES,)), dma((PIECES,)),
+        ],
+        compiler_params=pltpu.CompilerParams(
+            collective_id=number, has_side_effects=True,
+            vmem_limit_bytes=60 * 1024 * 1024,
+        ),
+    )(ztab, xtab, otab, blocks)
+
+
+def settle_levels(planes, blk_dev):
+    def pad(first, second):
+        return ((first, second) + (0,) * planes)[: planes - 1]
+
+    few = blk_dev * 3 // 4
+    pairs = [(f, s) for f in range(blk_dev // 2, few + 1) for s in range(blk_dev // 2, few + 1)]
+    pairs = sorted((f + 2 * s, pad(f, s), few) for f, s in pairs if abs(f - s) < 2 or s < f or f == s)
+    return [(c, cx) for _, c, cx in pairs] + [((blk_dev,) * (planes - 1), blk_dev)]
+
+
+def pack(blocks, keep_all, me, count, blk_dev, first_id):
+    i32 = jnp.int32
+    planes = count // 2
+    plane, side = me // 2, me % 2
+    index = jnp.arange(count * blk_dev, dtype=i32)
+    kept = keep_all > 0
+    rank = exclusive(keep_all, 0)
+    source, goal = index // blk_dev, rank // blk_dev
+    far = source // 2 - goal // 2
+    earlier = index[None] < index[:, None]
+    same_z = (source[:, None] == source[None]) & (far[:, None] == far[None])
+    by_z = jnp.sum((earlier & same_z & kept[None]).astype(i32), axis=1)
+    crosses = kept & (source % 2 != goal % 2)
+    same_x = (goal[:, None] // 2 == goal[None] // 2) & (source[:, None] % 2 == source[None] % 2)
+    by_x = jnp.sum((earlier & same_x & crosses[None]).astype(i32), axis=1)
+    deltas = jnp.arange(1, planes, dtype=i32)
+    of_delta = kept[None] & (far[None] == deltas[:, None])
+    most_z = jnp.max(of_delta * (by_z + 1)[None], axis=1)
+    most_x = jnp.max(crosses * (by_x + 1))
+    choices = settle_levels(planes, blk_dev)
+    caps = jnp.asarray([c for c, _ in choices], i32)
+    caps_x = jnp.asarray([c for _, c in choices], i32)
+    enough = jnp.all(most_z[None] <= caps, axis=1) & (most_x <= caps_x)
+    level = jnp.argmax(enough).astype(i32)
+    own_caps = caps[level]
+    base = blk_dev + exclusive(own_caps, 0)
+    base = jnp.sum((far[:, None] == deltas[None]).astype(i32) * base[None], axis=1)
+    held = jnp.where(far == 0, index % blk_dev, base + by_z)
+
+    def listed(flags, places, worth, cap):
+        hit = (flags[..., None, :] & (places == jnp.arange(cap, dtype=i32)[:, None])).astype(i32)
+        return jnp.sum(hit * worth, axis=-1)
+
+    ztab = listed(of_delta & (source == me)[None], by_z, index % blk_dev, blk_dev)
+    comes = crosses & (goal // 2 == plane) & (source % 2 == side)
+    xtab = listed(comes, by_x, held, blk_dev)[None]
+    lands = kept & (goal == me)
+    straight = source % 2 == side
+    kind = jnp.where(straight, 1, 2)
+    worth = jnp.stack([kind, jnp.where(straight, held, 0), jnp.where(straight, 0, by_x)])
+    hit = (lands & (rank % blk_dev == jnp.arange(blk_dev, dtype=i32)[:, None])).astype(i32)
+    otab = jnp.sum(hit[None] * worth[:, None], axis=-1)
+
+    def run(number, caps, cx):
+        return lambda *args: settled(count, first_id + number, caps, cx, blk_dev, *args)
+
+    runs = [run(n, c, cx) for n, (c, cx) in enumerate(choices)]
+    return lax.switch(level, runs, ztab, xtab, otab, blocks)
+
+
 CHUNK = 8
 
 
 def near_far_kernel(
-    blk_dev, keep_ref, slot_ref, live_ref, where_ref, used_ref,
+    blk_dev, keep_ref, live_ref, where_ref, used_ref,
     q_ref, k_ref, v_ref, hk_ref, hv_ref, gk_ref, gv_ref, rand_hbm, out_ref, rand_ref, sems,
 ):
     scale = 1.0 / math.sqrt(DH)
@@ -584,8 +793,6 @@
             pl.when(c * CHUNK < used_ref[0])(lambda c=c: copy(c).start())
         for c in range(chunks):
             pl.when(c * CHUNK < used_ref[0])(lambda c=c: copy(c).wait())
-
-    out_ref[...] = jnp.zeros_like(out_ref)
 
     def tile(ref, halo_ref, i):
         if i < 0:
@@ -631,14 +838,13 @@
             w = jnp.exp(s - peak).astype(jnp.bfloat16)
             denom = denom + jnp.sum(w.astype(jnp.float32), axis=-1, keepdims=True)
             numer = numer + jnp.dot(w, v, preferred_element_type=jnp.float32)
-        rows = pl.ds(pl.multiple_of(slot_ref[i] * B, B), B)
-        out_ref[rows, :] = (numer / denom).astype(out_ref.dtype)
+        out_ref[i * B : (i + 1) * B, :] = (numer / denom).astype(out_ref.dtype)
 
     for i in range(blk_dev):
         pl.when(keep_ref[i] > 0)(functools.partial(one, i))
 
 
-def near_far(keep, slot, live, where, used, q, k, v, halo_kv, glob, rand):
+def near_far(keep, live, where, used, q, k, v, halo_kv, glob, rand):
     tok_dev, width_dev = q.shape
     blk_dev, head_dev = tok_dev // B, width_dev // DH
 
@@ -652,7 +858,7 @@
         functools.partial(near_far_kernel, blk_dev),
         out_shape=jax.ShapeDtypeStruct(q.shape, q.dtype),
         grid_spec=pltpu.PrefetchScalarGridSpec(
-            num_scalar_prefetch=5,
+            num_scalar_prefetch=4,
             grid=(head_dev,),
             in_specs=[column(tok_dev)] * 3
             + [part(2 * B, 0), part(2 * B, 1), part(G * B, 0), part(G * B, 1)]
@@ -664,7 +870,7 @@
             ],
         ),
         compiler_params=ANYWHERE,
-    )(keep, slot, live, where, used, q, k, v, halo_kv, halo_kv, glob, glob, rand)
+    )(keep, live, where, used, q, k, v, halo_kv, halo_kv, glob, glob, rand)
 
 
 def levels(tiles, most):
@@ -687,7 +893,7 @@
     tiles = head_dev * blk_dev
     most = min(tiles, head_dev * max(2, (count_req + count - 1) // count))
     planes = count // 2
-    if count % 2 or planes < 2 or not fits(planes, tiles, most):
+    if count % 2 or planes % 2 or not fits(planes, tiles, most):
         return plain_body(queries, keys, values, random_holder, random_offset, keep)
     me = lax.axis_index("seq")
     plane, side = me // 2, me % 2
@@ -777,16 +983,11 @@
         level, [exchanged(n, c) for n, c in enumerate(caps)], ztab, xtab, keys, values
     )
 
-    rank = exclusive(keep_all, 0)
-    slot = rank % blk_dev
-    source = jnp.arange(count * blk_dev, dtype=i32) // blk_dev
-    distance = jnp.where(keep_all > 0, source - rank // blk_dev, 0)
-    my_slots = lax.dynamic_slice_in_dim(slot, me * blk_dev, blk_dev)
     live = jnp.stack([me > 0, me < count - 1]).astype(i32)
     blocks = near_far(
-        keep, my_slots, live, where, used[None], queries, keys, values, halo_kv, glob, rand
+        keep, live, where, used[None], queries, keys, values, halo_kv, glob, rand
     )
-    return settle(blocks, keep_all, slot, source, distance, me, count, blk_dev)
+    return pack(blocks, keep_all, me, count, blk_dev, len(caps))
 
 
 def solution(mesh):

time: 545 us -> 418 us (0.77)
  the two profiles are of different devices: /device:TPU:10 before, /device:TPU:0 now
where the time goes in v1:
time: 418 us; the launch traced here: 415 us
  Pallas kernels  362 us (87%)
  other arithmetic  17.5 us (4%)
  local copies, waits for them, and re-layouts  13.6 us (3%)
  between operations  7.57 us (2%)
  starting transfers between devices  7.33 us (2%)
  waiting for transfers between devices  6.19 us (1%)
    pallas_call x1, Pallas kernels, exchange(): pl.pallas_call(functools.partial(exchange_kernel, count, cz, cx, blk_dev)...  232 us
    pallas_call x1, Pallas kernels, settled(): pl.pallas_call(functools.partial(settle_kernel, count, caps, cx, blk_dev)...  108 us
    pallas_call x1, Pallas kernels, near_far(): pl.pallas_call(functools.partial(near_far_kernel, blk_dev), out_shape=jax...  21.8 us
  transfers between devices with their start and end apart: 1, of which 1 were waited for; matrix products, arithmetic and copies ran while one was open for 0% of the time, Pallas kernels for 0%

profile of v1, /device:TPU:0, one launch (start us, length us, event | category | flops | bytes accessed | tf_op | source)
XLA Modules:
  0.0 414.9 jit_solution(13427682815325524491)
XLA Ops:
  0.0 0.7 compare_and_fusion.20
  0.7 0.7 broadcast_select_fusion
  1.4 0.1 copy.64
  1.5 0.1 reshape.916
  1.7 0.7 pad_add_fusion.4
  2.4 0.6 broadcast_in_dim.68
  3.0 7.3 %all-to-all-start = ((s32[32,1,200]{2,1,0:T(1,128)}), s32[32,1,200]{2,1,0:T(1,128)S(1)}, u32[]{:S(2)}, u32[]{:S(2)}) async-start(s32[32,1,200]{2,1,0:T(1,128)} %broadcast_in_dim.68), calls=%async_computation | async-start | bytes 65536 | tf_op jit(solution)/shard_map/all_to_all | solution.py:907
  10.5 0.1 compare_and_fusion.19
  10.6 0.7 add_convert_fusion.live_ref
  11.4 6.2 %all-to-all-done = s32[32,1,200]{2,1,0:T(1,128)S(1)} async-done(((s32[32,1,200]{2,1,0:T(1,128)}), s32[32,1,200]{2,1,0:T(1,128)S(1)}, u32[]{:S(2)}, u32[]{:S(2)}) %all-to-all-start) | async-done | bytes 25632 | tf_op jit(solution)/shard_map/all_to_all | solution.py:907
  17.6 0.1 reduce.21
  17.7 0.1 fusion.36
  17.8 0.1 reshape_squeeze.5
  18.0 0.1 reduce-window.6
  18.1 0.1 reduce.24
  18.2 0.1 reshape.920
  18.3 0.1 eq.361
  18.4 1.4 convert_reduce_fusion
  19.8 0.3 reshape_reshape.3
  20.2 1.3 reshape.923
  21.5 0.1 reduce_sum.126
  21.6 0.6 reduce_sum.127
  22.3 0.9 reduce_max.57
  23.2 0.6 reduce_max.59
  23.9 1.4 reduce_sum.124
  25.3 0.6 fusion.17
  25.9 1.1 compare_or_fusion
  27.1 0.7 fusion.27
  29.6 0.6 dynamic_slice.51
  30.2 0.7 dynamic_slice.50
  31.5 0.9 dynamic-slice_bitcast_fusion.1
  32.5 0.1 reshape.922
  32.6 0.1 convolution_convert_fusion.1
  32.7 1.0 dynamic-slice_bitcast_fusion
  33.8 0.1 reshape.924
  33.9 0.1 convolution_convert_fusion
  34.1 0.2 convert_reduce_fusion.1
  34.3 0.1 reshape_squeeze.6
  34.4 0.2 convert_reduce_fusion.2
  34.6 0.2 select_reduce_fusion.20
  34.9 0.1 compare_reduce_fusion
  35.0 0.7 fusion.23
  35.7 1.4 and_reduce_fusion
  39.9 1.2 compare_select_fusion.47
  41.1 0.1 add_bitcast_fusion
  41.3 0.3 select_reduce_fusion.18
  41.6 0.6 min.10.where_ref
  42.8 0.6 gather_fusion
  43.4 0.6 gather_fusion.1
  43.9 0.6 gather_fusion.2
  44.5 0.6 gather_fusion.3
  45.0 0.6 gather_fusion.4
  47.0 0.2 reduce-window_1_clone.1
  47.2 0.1 select_reduce_fusion.19
  47.5 0.1 multiply_reduce_fusion.9
  47.6 0.2 multiply_reduce_fusion.10
  47.8 232.7 %conditional.2 = ((bf16[312,256,128]{2,1,0:T(8,128)(2,1)}, bf16[2,256,1024]{2,1,0:T(8,128)(2,1)S(1)}, bf16[2,256,1024]{2,1,0:T(8,128)(2,1)})) conditional(s32[]{:T(128)} %clamp.19, (s32[3,64]{1,0:T(4,128)S(1)}, s32[5,24]{1,0:T(8,128)S(1)}, bf16[1024,1024]{1,0:T(8,128)(2,1)S(1)}, ...), branch_computations={%region_23.26_spmd, %region_24.27_spmd, %region_25.28_spmd, %regio... | conditional | bytes 8 | solution.py:982
  47.8 232.5 %branch_4_fun.2 = (bf16[312,256,128]{2,1,0:T(8,128)(2,1)}, bf16[2,256,1024]{2,1,0:T(8,128)(2,1)S(1)}, bf16[2,256,1024]{2,1,0:T(8,128)(2,1)}) custom-call(s32[3,64]{1,0:T(4,128)S(1)} %get-tuple-element.169.ztab, s32[5,24]{1,0:T(8,128)S(1)} %get-tuple-element.170.xtab, bf16[1024,1024]{1,0:T(8,128)(2,1)S(1)} %get-tuple-element.171.k_ref, ...), custom_call_target="tpu_custom_call" | custom-call | tf_op jit(solution)/shard_map/cond/branch_4_fun/pallas_call | solution.py:557
  280.6 21.8 %shard_map.118 = bf16[1024,1024]{1,0:T(8,128)(2,1)S(1)} custom-call(s32[8]{0:T(128)} %keep_ref.1, s32[2]{0:T(128)} %add_convert_fusion.live_ref, s32[192]{0:T(256)} %min.10.where_ref, s32[1]{0:T(128)} %bitcast.12.used_ref, bf16[1024,1024]{1,0:T(8,128)(2,1)} %q_ref.1, bf16[1024,1024]{1,0:T(8,128)(2,1)} %k_ref.1, bf16[1024,1024]{1,0:T(8,128)(2,1)} %v_ref.1, ...), custom_call_target="tpu_custom_call" | custom-call | tf_op jit(solution)/shard_map/pallas_call | solution.py:857
  302.4 109.4 %conditional.3 = (bf16[1024,1024]{1,0:T(8,128)(2,1)}) conditional(s32[]{:T(128)} %clamp.18, (pred[3,64]{1,0:T(4,128)(4,1)S(1)}, pred[64]{0:T(512)(128)(4,1)S(1)}, s32[8,64]{1,0:T(8,128)S(1)}, bf16[1024,1024]{1,0:T(8,128)(2,1)S(1)}, s32[]{:T(128)}, /*index=5*/s32[64]{0:T(128)S(1)}, s32[]{:T(128)}, ...), branch_computations={%region_31.34_spmd.clone, %region_32.35_spmd.clone, %region_33.36_... | conditional | flops 10824 | bytes 12416 | solution.py:772
  302.5 0.8 multiply_reduce_fusion.1
  303.3 0.7 select_reduce_fusion.3
  303.9 107.9 %branch_1_fun.3 = bf16[1024,1024]{1,0:T(8,128)(2,1)} custom-call(s32[3,8]{1,0:T(4,128)} %get-tuple-element.1157.ztab, s32[1,8]{1,0:T(1,128)} %bitcast.72, s32[3,8]{1,0:T(4,128)} %get-tuple-element.1156.otab, bf16[1024,1024]{1,0:T(8,128)(2,1)S(1)} %get-tuple-element.763.in_ref), custom_call_target="tpu_custom_call" | custom-call | tf_op jit(solution)/shard_map/cond/branch_1_fun/pallas_call | solution.py:695
  411.8 3.1 copy.115
  (73 shorter events, 1.2 us)
Async XLA Ops:
  3.0 14.6 %all-to-all-start = ((s32[32,1,200]{2,1,0:T(1,128)}), s32[32,1,200]{2,1,0:T(1,128)S(1)}, u32[]{:S(2)}, u32[]{:S(2)}) async-start(s32[32,1,200]{2,1,0:T(1,128)} %broadcast_in_dim.68), calls=%async_computation | async-start | bytes 65536 | tf_op jit(solution)/shard_map/all_to_all | solution.py:907
  11.4 11.8 %copy-start.2 = (s32[5,64]{1,0:T(8,128)}, s32[5,64]{1,0:T(8,128)S(1)}, u32[]{:S(2)}) copy-start(s32[5,64]{1,0:T(8,128)S(1)} %broadcast_in_dim.73) | copy-start | bytes 3844
  20.2 5.8 %copy-start.4 = (s32[8]{0:T(128)S(1)}, s32[8]{0:T(128)}, u32[]{:S(2)}) copy-start(s32[8]{0:T(128)} %constant.384.clone) | copy-start | bytes 100
  20.2 5.7 %copy-start.5 = (s32[8]{0:T(128)S(1)}, s32[8]{0:T(128)}, u32[]{:S(2)}) copy-start(s32[8]{0:T(128)} %constant.385.clone) | copy-start | bytes 100
  22.3 12.6 %copy-start.1 = (s32[9,3]{1,0:T(8,128)S(1)}, s32[9,3]{1,0:T(8,128)}, u32[]{:S(2)}) copy-start(s32[9,3]{1,0:T(8,128)} %constant.386.clone) | copy-start | bytes 328
  22.3 13.5 %copy-start.3 = (s32[9]{0:T(128)S(1)}, s32[9]{0:T(128)}, u32[]{:S(2)}) copy-start(s32[9]{0:T(128)} %constant.387.clone) | copy-start | bytes 112
  22.3 25.5 %copy-start = (bf16[1024,1024]{1,0:T(8,128)(2,1)S(1)}, bf16[1024,1024]{1,0:T(8,128)(2,1)}, u32[]{:S(2)}) copy-start(bf16[1024,1024]{1,0:T(8,128)(2,1)} %k_ref.1) | copy-start | bytes 6291460
  23.9 23.6 %slice-start = ((s32[5,64]{1,0:T(8,128)}), s32[3,64]{1,0:T(4,128)S(1)}, s32[]{:S(2)}) async-start(s32[5,64]{1,0:T(8,128)} %copy-done.2), calls=%async_computation.1 | async-start | bytes 4096 | tf_op jit(solution)/shard_map/slice | solution.py:948

commit v2 on v1

--- a/solution.py
+++ b/solution.py
@@ -584,8 +584,8 @@
 
 
 def settle_kernel(
-    count, caps, cx, blk_dev, ztab, xtab, otab, in_ref, out_ref,
-    mine, zs, pool, xs, xr, z_send, z_recv, x_send, x_recv,
+    count, caps, cr, cx, blk_dev, ztab, rtab, xtab, otab, in_ref, out_ref,
+    mine, zs, pool, rs, xs, xr, z_send, z_recv, r_send, r_recv, x_send, x_recv,
 ):
     planes = count // 2
     me = lax.axis_index("seq")
@@ -609,6 +609,9 @@
     used = [d for d in range(1, planes) if caps[d - 1] > 0]
     used.sort(reverse=True)
     base = {d: blk_dev + sum(caps[: d - 1]) for d in used}
+    gate = planes // 2 - 1
+    beyond = range(1, gate + 1)
+    r_base = blk_dev + sum(caps)
 
     def fill(dst, src, table, row, cap):
         def one(j, carry):
@@ -635,6 +638,12 @@
                 z_send.at[piece, n], z_recv.at[piece, n],
                 jnp.maximum(me - 2 * d, 0),
             )
+        for d in beyond:
+            z_copies[piece, -d] = remote(
+                rs[piece][d - 1], pool[piece].at[pl.ds(r_base, cr)],
+                r_send.at[piece, d - 1], r_recv.at[piece],
+                jnp.maximum(me - 2 * d, 0),
+            )
         x_copies.append(remote(xs[piece], xr[piece], x_send.at[piece], x_recv.at[piece], mate))
     def start_z(piece):
         for d in used:
@@ -668,6 +677,18 @@
             @pl.when(plane + d < planes)
             def _(d=d, piece=piece):
                 z_copies[piece, d].wait_recv()
+
+        @pl.when(plane == gate)
+        def _(piece=piece):
+            for d in beyond:
+                fill(rs[piece][d - 1], pool[piece], rtab, d - 1, cr)
+                z_copies[piece, -d].start()
+
+        @pl.when(plane < gate)
+        def _(piece=piece):
+            if gate > 0:
+                z_copies[piece, -1].wait_recv()
+
         fill(xs[piece], pool[piece], xtab, 0, cx)
         x_copies[piece].start()
         if piece > 0:
@@ -680,8 +701,13 @@
             def _(d=d, piece=piece):
                 z_copies[piece, d].wait_send()
 
-
-def settled(count, number, caps, cx, blk_dev, ztab, xtab, otab, blocks):
+        @pl.when(plane == gate)
+        def _(piece=piece):
+            for d in beyond:
+                z_copies[piece, -d].wait_send()
+
+
+def settled(count, number, caps, cr, cx, blk_dev, ztab, rtab, xtab, otab, blocks):
     tok, width = blocks.shape
     planes, wide = count // 2, width // PIECES
     smem = pl.BlockSpec(memory_space=pltpu.SMEM)
@@ -693,33 +719,41 @@
         return [pltpu.VMEM((rows, B, wide), dtype) for _ in range(PIECES)]
 
     return pl.pallas_call(
-        functools.partial(settle_kernel, count, caps, cx, blk_dev),
+        functools.partial(settle_kernel, count, caps, cr, cx, blk_dev),
         out_shape=jax.ShapeDtypeStruct(blocks.shape, dtype),
-        in_specs=[smem, smem, smem, vmem],
+        in_specs=[smem, smem, smem, smem, vmem],
         out_specs=vmem,
         scratch_shapes=[
             each(blk_dev),
             [[pltpu.VMEM((c, B, wide), dtype) for c in sent] for _ in range(PIECES)],
-            each(blk_dev + sum(caps)),
+            each(blk_dev + sum(caps) + cr),
+            [[pltpu.VMEM((cr, B, wide), dtype) for _ in range(planes // 2 - 1)] for _ in range(PIECES)],
             each(cx),
             each(cx),
-            dma((PIECES, len(sent))), dma((PIECES, len(sent))), dma((PIECES,)), dma((PIECES,)),
+            dma((PIECES, len(sent))), dma((PIECES, len(sent))),
+            dma((PIECES, planes // 2)), dma((PIECES,)), dma((PIECES,)), dma((PIECES,)),
         ],
         compiler_params=pltpu.CompilerParams(
             collective_id=number, has_side_effects=True,
             vmem_limit_bytes=60 * 1024 * 1024,
         ),
-    )(ztab, xtab, otab, blocks)
+    )(ztab, rtab, xtab, otab, blocks)
 
 
 def settle_levels(planes, blk_dev):
     def pad(first, second):
         return ((first, second) + (0,) * planes)[: planes - 1]
 
-    few = blk_dev * 3 // 4
-    pairs = [(f, s) for f in range(blk_dev // 2, few + 1) for s in range(blk_dev // 2, few + 1)]
-    pairs = sorted((f + 2 * s, pad(f, s), few) for f, s in pairs if abs(f - s) < 2 or s < f or f == s)
-    return [(c, cx) for _, c, cx in pairs] + [((blk_dev,) * (planes - 1), blk_dev)]
+    half, few = blk_dev // 2, blk_dev * 3 // 4
+    choices = [
+        (2 * max(f + t, f + r) + r, pad(f, t), r, few)
+        for f in range(half, few + 1)
+        for t in range(half, few + 1)
+        for r in (half // 2, half)
+        if abs(f - t) < 2 or t == half
+    ]
+    choices = sorted(choices) + [(0, (blk_dev,) * (planes - 1), blk_dev, blk_dev)]
+    return [limits for _, *limits in choices]
 
 
 def pack(blocks, keep_all, me, count, blk_dev, first_id):
@@ -730,10 +764,14 @@
     kept = keep_all > 0
     rank = exclusive(keep_all, 0)
     source, goal = index // blk_dev, rank // blk_dev
-    far = source // 2 - goal // 2
+    gate = planes // 2 - 1
+    relayed = kept & (source // 2 == gate + 1) & (goal // 2 < gate)
+    far = jnp.where(relayed, 1, source // 2 - goal // 2)
     earlier = index[None] < index[:, None]
     same_z = (source[:, None] == source[None]) & (far[:, None] == far[None])
     by_z = jnp.sum((earlier & same_z & kept[None]).astype(i32), axis=1)
+    same_r = (goal[:, None] // 2 == goal[None] // 2) & (source[:, None] % 2 == source[None] % 2)
+    by_r = jnp.sum((earlier & same_r & relayed[None]).astype(i32), axis=1)
     crosses = kept & (source % 2 != goal % 2)
     same_x = (goal[:, None] // 2 == goal[None] // 2) & (source[:, None] % 2 == source[None] % 2)
     by_x = jnp.sum((earlier & same_x & crosses[None]).astype(i32), axis=1)
@@ -741,21 +779,27 @@
     of_delta = kept[None] & (far[None] == deltas[:, None])
     most_z = jnp.max(of_delta * (by_z + 1)[None], axis=1)
     most_x = jnp.max(crosses * (by_x + 1))
+    most_r = jnp.max(relayed * (by_r + 1))
     choices = settle_levels(planes, blk_dev)
-    caps = jnp.asarray([c for c, _ in choices], i32)
-    caps_x = jnp.asarray([c for _, c in choices], i32)
-    enough = jnp.all(most_z[None] <= caps, axis=1) & (most_x <= caps_x)
+    caps = jnp.asarray([c for c, _, _ in choices], i32)
+    caps_r = jnp.asarray([c for _, c, _ in choices], i32)
+    caps_x = jnp.asarray([c for _, _, c in choices], i32)
+    enough = jnp.all(most_z[None] <= caps, axis=1) & (most_x <= caps_x) & (most_r <= caps_r)
     level = jnp.argmax(enough).astype(i32)
     own_caps = caps[level]
     base = blk_dev + exclusive(own_caps, 0)
     base = jnp.sum((far[:, None] == deltas[None]).astype(i32) * base[None], axis=1)
-    held = jnp.where(far == 0, index % blk_dev, base + by_z)
+    first = jnp.where(far == 0, index % blk_dev, base + by_z)
+    held = jnp.where(relayed, blk_dev + jnp.sum(own_caps) + by_r, first)
 
     def listed(flags, places, worth, cap):
         hit = (flags[..., None, :] & (places == jnp.arange(cap, dtype=i32)[:, None])).astype(i32)
         return jnp.sum(hit * worth, axis=-1)
 
     ztab = listed(of_delta & (source == me)[None], by_z, index % blk_dev, blk_dev)
+    hops = jnp.arange(1, max(gate, 1) + 1, dtype=i32)
+    passes = relayed & (source % 2 == side) & (plane == gate)
+    rtab = listed(passes[None] & (gate - goal // 2 == hops[:, None]), by_r, first, blk_dev)
     comes = crosses & (goal // 2 == plane) & (source % 2 == side)
     xtab = listed(comes, by_x, held, blk_dev)[None]
     lands = kept & (goal == me)
@@ -765,11 +809,11 @@
     hit = (lands & (rank % blk_dev == jnp.arange(blk_dev, dtype=i32)[:, None])).astype(i32)
     otab = jnp.sum(hit[None] * worth[:, None], axis=-1)
 
-    def run(number, caps, cx):
-        return lambda *args: settled(count, first_id + number, caps, cx, blk_dev, *args)
-
-    runs = [run(n, c, cx) for n, (c, cx) in enumerate(choices)]
-    return lax.switch(level, runs, ztab, xtab, otab, blocks)
+    def run(number, *limits):
+        return lambda *args: settled(count, first_id + number, *limits, blk_dev, *args)
+
+    runs = [run(n, *limits) for n, limits in enumerate(choices)]
+    return lax.switch(level, runs, ztab, rtab, xtab, otab, blocks)
 
 
 CHUNK = 8

time: 418 us -> 450 us (1.077)
  Pallas kernels: 362 us -> 395 us
    pallas_call x1, Pallas kernels: 108 us -> 122 us  [settled(): pl.pallas_call(functools.partial(settle_kernel, count, caps, cr, cx, blk_...]
    pallas_call x1, Pallas kernels: 232 us -> 247 us  [exchange(): pl.pallas_call(functools.partial(exchange_kernel, count, cz, cx, blk_dev)...]
    pallas_call x1, Pallas kernels: 21.8 us -> 26.4 us  [near_far(): pl.pallas_call(functools.partial(near_far_kernel, blk_dev), out_shape=jax...]
where the time goes in v2:
time: 450 us; the launch traced here: 451 us
  Pallas kernels  395 us (88%)
  other arithmetic  19.6 us (4%)
  local copies, waits for them, and re-layouts  13.7 us (3%)
  between operations  8.17 us (2%)
  starting transfers between devices  7.33 us (2%)
  waiting for transfers between devices  6.23 us (1%)
    pallas_call x1, Pallas kernels, exchange(): pl.pallas_call(functools.partial(exchange_kernel, count, cz, cx, blk_dev)...  247 us
    pallas_call x1, Pallas kernels, settled(): pl.pallas_call(functools.partial(settle_kernel, count, caps, cr, cx, blk_...  122 us
    pallas_call x1, Pallas kernels, near_far(): pl.pallas_call(functools.partial(near_far_kernel, blk_dev), out_shape=jax...  26.4 us
  transfers between devices with their start and end apart: 1, of which 1 were waited for; matrix products, arithmetic and copies ran while one was open for 0% of the time, Pallas kernels for 0%

profile of v2, /device:TPU:0, one launch (start us, length us, event | category | flops | bytes accessed | tf_op | source)
XLA Modules:
  0.0 450.9 jit_solution(14996342665399537183)
XLA Ops:
  0.0 0.7 compare_and_fusion.36
  0.7 0.7 broadcast_select_fusion
  1.4 0.1 copy.85
  1.5 0.1 reshape.1228
  1.7 0.7 pad_add_fusion.4
  2.4 0.6 broadcast_in_dim.207
  3.0 7.3 %all-to-all-start = ((s32[32,1,200]{2,1,0:T(1,128)}), s32[32,1,200]{2,1,0:T(1,128)S(1)}, u32[]{:S(2)}, u32[]{:S(2)}) async-start(s32[32,1,200]{2,1,0:T(1,128)} %broadcast_in_dim.207), calls=%async_computation | async-start | bytes 65536 | tf_op jit(solution)/shard_map/all_to_all | solution.py:951
  10.5 0.1 compare_and_fusion.35
  10.6 0.6 add_convert_fusion.live_ref
  11.4 6.2 %all-to-all-done = s32[32,1,200]{2,1,0:T(1,128)S(1)} async-done(((s32[32,1,200]{2,1,0:T(1,128)}), s32[32,1,200]{2,1,0:T(1,128)S(1)}, u32[]{:S(2)}, u32[]{:S(2)}) %all-to-all-start) | async-done | bytes 25632 | tf_op jit(solution)/shard_map/all_to_all | solution.py:951
  17.9 0.1 reduce-window.6
  18.0 0.1 reduce.61
  18.2 0.1 and_select_fusion.5
  18.4 0.2 convert_reduce_fusion.2
  18.6 0.1 reshape_squeeze.6
  18.7 0.1 eq.1177
  18.8 1.4 convert_reduce_fusion
  20.2 0.3 reshape_reshape.3
  20.6 1.3 reshape.1235
  21.9 0.1 reduce_sum.518
  22.0 0.6 reduce_sum.522
  22.7 0.9 reduce_max.67
  23.7 0.6 reduce_max.69
  24.3 1.4 reduce_sum.516
  25.7 0.7 fusion.24
  26.4 1.2 compare_or_fusion
  27.6 0.7 fusion.33
  30.2 0.6 dynamic_slice.51
  30.8 0.7 dynamic_slice.50
  32.1 0.9 dynamic-slice_bitcast_fusion.1
  33.0 0.1 reshape.1234
  33.1 0.1 convolution_convert_fusion.1
  33.3 1.0 dynamic-slice_bitcast_fusion
  34.4 0.1 reshape.1236
  34.5 0.1 convolution_convert_fusion
  34.7 0.2 convert_reduce_fusion.3
  34.9 0.1 add.734
  35.0 0.2 select_reduce_fusion.53
  35.2 0.1 compare_reduce_fusion
  35.4 0.7 fusion.28
  36.1 1.9 and_reduce_fusion
  40.7 0.2 reduce-window_1_clone.1
  40.9 0.6 add_bitcast_fusion.1
  42.2 0.1 select_reduce_fusion.52
  43.7 1.2 compare_select_fusion.57
  44.9 0.1 add_bitcast_fusion
  45.1 0.3 select_reduce_fusion.51
  45.4 0.6 min.10.where_ref
  46.6 0.6 gather_fusion
  47.1 0.6 gather_fusion.1
  47.7 0.6 gather_fusion.2
  48.3 0.6 gather_fusion.3
  48.8 0.6 gather_fusion.4
  49.6 0.1 multiply_reduce_fusion.17
  49.7 0.2 multiply_reduce_fusion.18
  49.9 246.8 %conditional.2 = ((bf16[312,256,128]{2,1,0:T(8,128)(2,1)}, bf16[2,256,1024]{2,1,0:T(8,128)(2,1)S(1)}, bf16[2,256,1024]{2,1,0:T(8,128)(2,1)})) conditional(s32[]{:T(128)} %clamp.19, (s32[3,64]{1,0:T(4,128)S(1)}, s32[5,24]{1,0:T(8,128)S(1)}, bf16[1024,1024]{1,0:T(8,128)(2,1)S(1)}, ...), branch_computations={%region_20.23_spmd, %region_21.24_spmd, %region_22.25_spmd, %regio... | conditional | bytes 8 | solution.py:1026
  50.0 246.5 %branch_5_fun.3 = (bf16[312,256,128]{2,1,0:T(8,128)(2,1)}, bf16[2,256,1024]{2,1,0:T(8,128)(2,1)S(1)}, bf16[2,256,1024]{2,1,0:T(8,128)(2,1)}) custom-call(s32[3,64]{1,0:T(4,128)S(1)} %get-tuple-element.2948.ztab, s32[5,24]{1,0:T(8,128)S(1)} %get-tuple-element.2949.xtab, bf16[1024,1024]{1,0:T(8,128)(2,1)S(1)} %get-tuple-element.2950.k_ref, ...), custom_call_target="tpu_custom_call" | custom-call | tf_op jit(solution)/shard_map/cond/branch_5_fun/pallas_call | solution.py:557
  296.8 26.4 %shard_map.143 = bf16[1024,1024]{1,0:T(8,128)(2,1)S(1)} custom-call(s32[8]{0:T(128)} %keep_ref.1, s32[2]{0:T(128)} %add_convert_fusion.live_ref, s32[192]{0:T(256)} %min.10.where_ref, s32[1]{0:T(128)} %bitcast.17.used_ref, bf16[1024,1024]{1,0:T(8,128)(2,1)} %q_ref.1, bf16[1024,1024]{1,0:T(8,128)(2,1)} %k_ref.1, bf16[1024,1024]{1,0:T(8,128)(2,1)} %v_ref.1, ...), custom_call_target="tpu_custom_call" | custom-call | tf_op jit(solution)/shard_map/pallas_call | solution.py:901
  323.2 124.6 %conditional.3 = (bf16[1024,1024]{1,0:T(8,128)(2,1)}) conditional(s32[]{:T(128)} %clamp.18, (s32[64]{0:T(128)S(1)}, s32[64]{0:T(128)S(1)}, pred[3,64]{1,0:T(4,128)(4,1)S(1)}, s32[64]{0:T(128)S(1)}, s32[8,64]{1,0:T(8,128)S(1)}, /*index=5*/s32[64]{0:T(128)S(1)}, pred[64]{0:T(512)(128)(4,1)S(1)}, s32[64]{0:T(128)S(1)}, ...), branch_computations={%region_31.38_spmd.clone, %region_36.43_spmd.clone, %region_41.48_... | conditional | flops 13569 | bytes 16614 | solution.py:816
  323.3 0.8 multiply_reduce_fusion.3
  324.1 0.7 select_reduce_fusion.11
  324.8 0.6 select_reduce_fusion.10
  325.4 122.4 %branch_3_fun.4 = bf16[1024,1024]{1,0:T(8,128)(2,1)} custom-call(s32[3,8]{1,0:T(4,128)} %get-tuple-element.4517.ztab, s32[1,8]{1,0:T(1,128)} %bitcast.109, s32[1,8]{1,0:T(1,128)} %bitcast.126, s32[3,8]{1,0:T(4,128)} %get-tuple-element.4516.otab, bf16[1024,1024]{1,0:T(8,128)(2,1)S(1)} %get-tuple-element.3620.in_ref), custom_call_target="tpu_custom_call" | custom-call | tf_op jit(solution)/shard_map/cond/branch_3_fun/pallas_call | solution.py:721
  447.8 3.1 copy.145
  (81 shorter events, 1.5 us)
Async XLA Ops:
  3.0 14.6 %all-to-all-start = ((s32[32,1,200]{2,1,0:T(1,128)}), s32[32,1,200]{2,1,0:T(1,128)S(1)}, u32[]{:S(2)}, u32[]{:S(2)}) async-start(s32[32,1,200]{2,1,0:T(1,128)} %broadcast_in_dim.207), calls=%async_computation | async-start | bytes 65536 | tf_op jit(solution)/shard_map/all_to_all | solution.py:951
  11.4 12.3 %copy-start.2 = (s32[5,64]{1,0:T(8,128)}, s32[5,64]{1,0:T(8,128)S(1)}, u32[]{:S(2)}) copy-start(s32[5,64]{1,0:T(8,128)S(1)} %broadcast_in_dim.211) | copy-start | bytes 3844
  20.6 5.8 %copy-start.5 = (s32[8]{0:T(128)S(1)}, s32[8]{0:T(128)}, u32[]{:S(2)}) copy-start(s32[8]{0:T(128)} %constant.474.clone) | copy-start | bytes 100
  20.6 5.8 %copy-start.6 = (s32[8]{0:T(128)S(1)}, s32[8]{0:T(128)}, u32[]{:S(2)}) copy-start(s32[8]{0:T(128)} %constant.475.clone) | copy-start | bytes 100
  22.7 12.6 %copy-start.1 = (s32[17,3]{1,0:T(8,128)S(1)}, s32[17,3]{1,0:T(8,128)}, u32[]{:S(2)}) copy-start(s32[17,3]{1,0:T(8,128)} %constant.476.clone) | copy-start | bytes 616
  22.7 13.4 %copy-start.3 = (s32[17]{0:T(128)S(1)}, s32[17]{0:T(128)}, u32[]{:S(2)}) copy-start(s32[17]{0:T(128)} %constant.477.clone) | copy-start | bytes 208
  22.7 13.4 %copy-start.4 = (s32[17]{0:T(128)S(1)}, s32[17]{0:T(128)}, u32[]{:S(2)}) copy-start(s32[17]{0:T(128)} %constant.478.clone) | copy-start | bytes 208
  22.7 27.2 %copy-start = (bf16[1024,1024]{1,0:T(8,128)(2,1)S(1)}, bf16[1024,1024]{1,0:T(8,128)(2,1)}, u32[]{:S(2)}) copy-start(bf16[1024,1024]{1,0:T(8,128)(2,1)} %k_ref.1) | copy-start | bytes 6291460
  24.3 25.3 %slice-start = ((s32[5,64]{1,0:T(8,128)}), s32[3,64]{1,0:T(4,128)S(1)}, s32[]{:S(2)}) async-start(s32[5,64]{1,0:T(8,128)} %copy-done.2), calls=%async_computation.1 | async-start | bytes 4096 | tf_op jit(solution)/shard_map/slice | solution.py:992
